TPU v7x, 32 devices: a whole 2x2x4 slice. The times are simulated.
32 devices in a mesh: tm: 4 (over z), space: 8 (over y, x, core).
Axes of the slice: x: 2, y: 2, z: 4, core: 2. Of those that a mesh axis runs over, the one named last changes fastest.
Arguments:
- eigvecs: bfloat16 [4, 128, 2, 3, 32, 512], P('tm', None, None, None, 'space'), may hold values from -0.29882812 to 0.29882812
- gauge_links: float32 [4, 3, 2, 3, 3, 32, 512], P('tm', None, None, None, None, 'space'), may hold values from -1 to 1, as said below
- perambulator: bfloat16 [8, 4, 2, 128, 128], P('tm'), may hold values from -0.375 to 0.375
- job_owner: int32 [96, 1], replicated, may hold values from 0 to 3; in each aligned block of 24 rows (0 to 23, 24 to 47, ...) at most 18 rows name the same one
- job_elemental: int32 [96], replicated, may hold values from 0 to 3
- job_source: int32 [96], replicated, may hold values from 0 to 1
- job_spin: int32 [96], replicated, may hold values from 0 to 3
Outputs:
- dressed: bfloat16 [4, 4, 18, 2, 128, 128], P('tm', None, None, None, 'space')
Inputs may be any that keep to these rules, and one draw needn't show every extreme that they name: `gauge_links`: each site's and direction's 3x3 complex matrix is special unitary. `job_owner`: jobs come in aligned blocks of 24 rows, block s holding the jobs of timeslice group s (timeslice s); within one block no owner is named by more than 18 rows, a bound that some block reaches. `job_elemental`: the job's timeslice within its group times 4 plus its operator (0 the momentum-projected plain elemental, 1 to 3 the derivatives along x1, x2, x3). `job_source`: the job's source time among its owner's 2 source times.
All inputs are finite; a program needn't handle non-finite values.
Results may differ from a plain program's by a relative error of at most 0.0057.
Values may be sent and summed in bfloat16 or wider, within the bound.
No kernel may reach another device: no remote copies, remote signals or barrier semaphores. Data moves between devices by JAX's collectives and lax.ppermute only.
A program may use at most 128 MiB of HBM per device.

v0:
```python
import math
from functools import partial

import numpy as np
import jax
import jax.numpy as jnp
from jax import lax
from jax.experimental import pallas as pl
from jax.experimental.pallas import tpu as pltpu
from jax.sharding import PartitionSpec as P

LY = 16
LZ = 32
OPS = 4
SPIN = 4
JOB_DEV = 24
LANES = 128
GROUP = 16
NARROW = (1, 2)
F32 = jnp.float32
BF16 = jnp.bfloat16
VMEM = pltpu.VMEM
SMEM = pltpu.SMEM


def vspec():
    return pl.BlockSpec(memory_space=VMEM)


def cost(flops, moved):
    return pl.CostEstimate(flops=flops, bytes_accessed=moved, transcendentals=0)


def limit(mebibytes):
    return pltpu.CompilerParams(vmem_limit_bytes=mebibytes * 2**20)


def pick_matrix(rows, cols, source_of):
    row = lax.broadcasted_iota(jnp.int32, (rows, cols), 0)
    col = lax.broadcasted_iota(jnp.int32, (rows, cols), 1)
    return jnp.where(col == source_of(row), 1.0, 0.0).astype(BF16)


def joined(pieces):
    return jnp.concatenate(pieces, axis=1)


def nt_dot(left, right):
    return lax.dot_general(left, right, (((1,), (1,)), ((), ())), preferred_element_type=F32)


def rim_kernel(tiles, planes, start, leads, x_hbm, u_hbm, *refs):
    if leads:
        out_ref, x_ref, link_ref, u_ref, pick_ref, sems = refs
    else:
        link_ref, out_ref, x_ref, u_ref, pick_ref, sems = refs
    spots = tiles * planes
    pair = 2
    part_count = out_ref.shape[2] // 2
    chunk = GROUP * 6 * spots
    chunks = part_count // GROUP
    rows_of = [pl.ds(g * chunk, chunk) for g in range(chunks)]
    copies = [
        pltpu.make_async_copy(x_hbm.at[pl.ds((start + g) * chunk, chunk)], x_ref.at[rows], sems.at[g])
        for g, rows in enumerate(rows_of)
    ]
    link_copy = pltpu.make_async_copy(u_hbm.at[pl.ds(0, u_ref.shape[0])], u_ref, sems.at[chunks])
    for copy in [link_copy] + copies if leads else copies + [link_copy]:
        copy.start()

    def source(row):
        return (row & (GROUP - 1)) * spots + (row // GROUP) * planes + planes - 1

    pick_ref[...] = pick_matrix(tiles * GROUP, GROUP * spots, source)
    if leads:
        link_copy.wait()
        for tile in range(tiles):
            flat = adjoint(load_rows(u_ref, 0, tile * planes + planes - 1, spots))
            for k, link in enumerate(flat):
                link_ref[tile, k] = link
    chosen = pick_ref[...]
    for g in range(chunks):
        copies[g].wait()
        block = x_ref[g * chunk : (g + 1) * chunk, :].reshape(GROUP, 6, spots, LANES)
        taken = []
        for part in range(0, 6, 2):
            rows = joined([block[:, part + k].reshape(GROUP * spots, LANES) for k in range(2)])
            got = jnp.dot(chosen, rows, preferred_element_type=F32)
            taken += [got[:, :LANES], got[:, LANES:]]
        for tile in range(tiles):
            links = [[[link_ref[tile, (p * 3 + r) * 3 + c] for c in range(3)] for r in range(3)] for p in range(3)]
            outs = []
            for eight in (0, 8):
                at = tile * GROUP + eight
                vec = [part[at : at + 8] for part in taken]
                outs.append(link_product(links, vec[:3], vec[3:]))
            for half in range(2):
                row = half * part_count + g * GROUP
                for colour in range(3):
                    both = jnp.concatenate([outs[0][half][colour], outs[1][half][colour]], axis=0)
                    out_ref[tile // pair, (tile % pair) * 3 + colour, row : row + GROUP] = both.astype(BF16)
    if not leads:
        link_copy.wait()


def lead_count(count):
    return count // (4 * GROUP) * GROUP


def rim_plane(x, u, links, count, tiles, planes):
    spots = tiles * planes
    pair = 2
    leads = links is None
    part_count = lead_count(count) if leads else count - lead_count(count)
    chunks = part_count // GROUP
    hbm = pl.BlockSpec(memory_space=pltpu.HBM)
    out_shape = [
        jax.ShapeDtypeStruct((tiles // pair, 3 * pair, 2 * part_count, LANES), BF16),
        jax.ShapeDtypeStruct((part_count * 6 * spots, LANES), BF16),
    ]
    scratch = [
        VMEM((tiles * GROUP, GROUP * spots), BF16),
        pltpu.SemaphoreType.DMA((chunks + 1,)),
    ]
    if leads:
        out_shape.append(jax.ShapeDtypeStruct((tiles, 27, 8, LANES), F32))
        scratch = [VMEM((18 * spots, LANES), F32)] + scratch
    else:
        out_shape.append(jax.ShapeDtypeStruct(u.shape, F32))
    return pl.pallas_call(
        partial(rim_kernel, tiles, planes, 0 if leads else lead_count(count) // GROUP, leads),
        in_specs=[hbm, hbm] + ([] if leads else [vspec()]),
        out_specs=[vspec()] * 3,
        out_shape=out_shape,
        scratch_shapes=scratch,
        compiler_params=limit(6),
        cost_estimate=cost(10**8, 2 * 10**6),
        name="rim" if leads else "rest",
    )(x, u, *([] if leads else [links]))


def link_product(links, vec_re, vec_im):
    plus = [vec_re[c] + vec_im[c] for c in range(3)]
    outs_re, outs_im = [], []
    for row in range(3):
        link_re, link_less, link_more = links[0][row], links[1][row], links[2][row]
        one = link_re[0] * plus[0] + link_re[1] * plus[1] + link_re[2] * plus[2]
        two = link_less[0] * vec_re[0] + link_less[1] * vec_re[1] + link_less[2] * vec_re[2]
        three = link_more[0] * vec_im[0] + link_more[1] * vec_im[1] + link_more[2] * vec_im[2]
        outs_re.append(one - three)
        outs_im.append(one + two)
    return outs_re, outs_im


def narrow_product(links, vec_re, vec_im):
    real, imag = links
    outs_re, outs_im = [], []
    for row in range(3):
        ones = [real[row][c] * vec_re[c] - imag[row][c] * vec_im[c] for c in range(3)]
        twos = [real[row][c] * vec_im[c] + imag[row][c] * vec_re[c] for c in range(3)]
        outs_re.append(ones[0] + ones[1] + ones[2])
        outs_im.append(twos[0] + twos[1] + twos[2])
    return outs_re, outs_im


def narrow_links(u_ref, direction, spot, spots):
    def one(part, row, col):
        at = (((direction * 2 + part) * 3 + row) * 3 + col) * spots + spot
        return jnp.broadcast_to(u_ref[pl.ds(at, 1), :], (GROUP, LANES)).astype(BF16)

    return [[[one(part, row, col) for col in range(3)] for row in range(3)] for part in range(2)]


def load_rows(u_ref, direction, spot, spots):
    def one(part, row, col):
        at = (((direction * 2 + part) * 3 + row) * 3 + col) * spots + spot
        return jnp.broadcast_to(u_ref[pl.ds(at, 1), :], (8, LANES))

    return [[[one(part, row, col) for col in range(3)] for row in range(3)] for part in range(2)]


def load_links(u_ref, direction, spot, spots):
    real, imag = load_rows(u_ref, direction, spot, spots)
    less = [[imag[row][col] - real[row][col] for col in range(3)] for row in range(3)]
    more = [[imag[row][col] + real[row][col] for col in range(3)] for row in range(3)]
    return real, less, more


def adjoint(grid):
    real, imag = grid
    order = [(row, col) for row in range(3) for col in range(3)]
    return (
        [real[col][row] for row, col in order]
        + [-imag[col][row] - real[col][row] for row, col in order]
        + [real[col][row] - imag[col][row] for row, col in order]
    )


def fill_table(groups, slots, empty, owner_ref, elem_ref, source_ref, spin_ref, table_ref):
    total = owner_ref.shape[1]
    jobs = total // groups
    row = lax.broadcasted_iota(jnp.int32, (total, total), 0)
    col = lax.broadcasted_iota(jnp.int32, (total, total), 1)

    def group_of(index):
        return sum((index >= group * jobs).astype(jnp.int32) for group in range(1, groups))

    live = jnp.where(owner_ref[...] == lax.axis_index("tm"), 1.0, 0.0)
    product = source_ref[...] * (SPIN * groups * OPS) + spin_ref[...] * (groups * OPS) + elem_ref[...]

    def column(mask, values):
        wide = jnp.broadcast_to(values.astype(F32), (total, total))
        return jnp.sum(jnp.where(mask, wide, 0.0), axis=1, keepdims=True)

    rank = column((col < row) & (group_of(col) == group_of(row)), live)
    alive = column(col == row, live)
    value = column(col == row, product)
    at_row = lax.broadcasted_iota(jnp.int32, (total, LANES), 0)
    at_col = lax.broadcasted_iota(jnp.int32, (total, LANES), 1)
    group = group_of(at_row).astype(F32)
    place = jnp.where(alive > 0.5, group * slots + rank, -1.0)
    found = at_col.astype(F32) == place
    picked = jnp.sum(jnp.where(found, value + group * OPS - empty, 0.0), axis=0, keepdims=True)
    table_ref[...] = (picked + empty).astype(jnp.int32)


def paired(grid, count):
    real = grid[:count, :count] + grid[count:, count:]
    imag = grid[count:, :count] - grid[:count, count:]
    return real, imag


def anti(real, imag):
    return 0.5 * (real.T - real), 0.5 * (imag.T + imag)


def gram_kernel(
    count, tiles, planes, lx, groups, slots, empty,
    low_ref, high_ref, u_ref, phase_ref, owner_ref, elem_ref, source_ref, spin_ref,
    sums_ref, rim_lhs_ref, table_ref,
    lhs_ref, op_ref, acc_ref, g_ref, pick_ref,
):
    spots = tiles * planes
    pair = 2
    halves = tiles // pair
    steps = planes * halves

    def source(row):
        spot = row // GROUP
        return (row & (GROUP - 1)) * spots + (spot % tiles) * planes + spot // tiles

    pick_ref[...] = pick_matrix(GROUP * spots, GROUP * spots, source)
    acc_ref[...] = jnp.zeros_like(acc_ref)
    g_ref[...] = jnp.zeros_like(g_ref)

    chosen = pick_ref[...]
    for at in range(0, count, GROUP):
        lead = lead_count(count)
        x_ref, near = (low_ref, at) if at < lead else (high_ref, at - lead)
        block = x_ref[near * 6 * spots : (near + GROUP) * 6 * spots, :].reshape(GROUP, 6, spots, LANES)
        for first in range(0, 6, 2):
            rows = jnp.concatenate(
                [block[:, first + k].reshape(GROUP * spots, LANES) for k in range(2)], axis=1
            )
            taken = jnp.dot(chosen, rows, preferred_element_type=F32)
            for k in range(2):
                part = first + k
                half, colour = part // 3, part % 3
                for spot in range(spots):
                    piece = taken[spot * GROUP : (spot + 1) * GROUP, k * LANES : (k + 1) * LANES]
                    plane, tile = spot // tiles, spot % tiles
                    lhs_ref[
                        plane * halves + tile // pair,
                        (tile % pair) * 3 + colour,
                        half * count + at : half * count + at + GROUP,
                    ] = piece.astype(BF16)

    lane = lax.broadcasted_iota(jnp.int32, (GROUP, LANES), 1)
    wraps = (lane & (LZ - 1)) == LZ - 1
    spills = lane < LZ

    def elementwise(step, slot, directions):
        plane = step // halves
        half_tile = step % halves
        for sub in range(pair):
            tile = half_tile * pair + sub
            ahead = step if sub + 1 < pair else plane * halves + (half_tile + 1) % halves
            for direction in directions:
                narrow = direction in NARROW
                links = (narrow_links if narrow else load_links)(
                    u_ref, direction, tile * planes + plane, spots
                )
                for at in range(0, count, GROUP):

                    def part(where, turn, k):
                        row = k // 3 * count + at
                        return lhs_ref[where, turn * 3 + k % 3, row : row + GROUP]

                    if direction == 0:
                        vec = [part(step + halves, sub, k) for k in range(6)]
                    elif direction == 1:
                        vec = [
                            pltpu.roll(
                                jnp.where(spills, part(ahead, (sub + 1) % pair, k), part(step, sub, k)), LANES - LZ, 1
                            )
                            for k in range(6)
                        ]
                    else:
                        vec = [
                            jnp.where(
                                wraps,
                                pltpu.roll(part(step, sub, k), LZ - 1, 1),
                                pltpu.roll(part(step, sub, k), LANES - 1, 1),
                            )
                            for k in range(6)
                        ]
                    if narrow:
                        outs = narrow_product(links, vec[:3], vec[3:])
                    else:
                        wide = [piece.astype(F32) for piece in vec]
                        pieces = [[piece[eight : eight + 8] for piece in wide] for eight in (0, 8)]
                        low, high = [link_product(links, piece[:3], piece[3:]) for piece in pieces]
                        outs = [
                            [
                                jnp.concatenate([low[half][colour], high[half][colour]], axis=0).astype(BF16)
                                for colour in range(3)
                            ]
                            for half in range(2)
                        ]
                    for half in range(2):
                        row = (direction * 2 + half) * count + at
                        for colour in range(3):
                            op_ref[slot, sub * 3 + colour, row : row + GROUP] = outs[half][colour]

    def multiply(step, slot, directions):
        fixed = joined([lhs_ref[step, k] for k in range(3 * pair)])
        low = min(directions) * 2 * count
        high = (max(directions) + 1) * 2 * count
        moving = joined([op_ref[slot, k, low:high] for k in range(3 * pair)])
        got = nt_dot(jnp.concatenate([fixed, moving], axis=0), fixed)
        g_ref[step // halves] += got[: 2 * count]
        acc_ref[low:high, :] += got[2 * count :]

    every, side = (0, 1, 2), (1, 2)
    inner = steps - halves
    elementwise(inner, 0, side)
    for step in range(inner + 1, steps):
        multiply(step - 1, (step - 1) & 1, side)
        elementwise(step, step & 1, side)
    multiply(steps - 1, (steps - 1) & 1, side)
    elementwise(0, 0, every)

    for step in range(1, inner):
        multiply(step - 1, (step - 1) & 1, every)
        elementwise(step, step & 1, every)
    multiply(inner - 1, (inner - 1) & 1, every)
    fill_table(groups, slots, empty, owner_ref, elem_ref, source_ref, spin_ref, table_ref)

    first = lax.axis_index("space") * planes
    place = lax.broadcasted_iota(jnp.int32, phase_ref.shape, 1)
    total_re = jnp.zeros((count, count), F32)
    total_im = jnp.zeros((count, count), F32)
    for plane in range(planes):
        real, imag = paired(g_ref[plane], count)
        cosine = jnp.sum(jnp.where(place == first + plane, phase_ref[...], 0.0), axis=1, keepdims=True)
        sine = jnp.sum(jnp.where(place == lx + first + plane, phase_ref[...], 0.0), axis=1, keepdims=True)
        total_re += cosine * real - sine * imag
        total_im += cosine * imag + sine * real
    sums_ref[0, 0] = total_re
    sums_ref[0, 1] = -total_im
    for direction in range(3):
        grid = acc_ref[direction * 2 * count : (direction + 1) * 2 * count, :]
        real, imag = anti(*paired(grid, count))
        sums_ref[direction + 1, 0] = real
        sums_ref[direction + 1, 1] = imag
    for half in range(halves):
        rim_lhs_ref[half] = lhs_ref[half]


def gram(low, high, u, phases, tables, count, tiles, planes, lx, groups, slots, empty):
    spots = tiles * planes
    pair = 2
    steps = planes * (tiles // pair)
    return pl.pallas_call(
        partial(gram_kernel, count, tiles, planes, lx, groups, slots, empty),
        in_specs=[vspec()] * 8,
        out_specs=[vspec()] * 3,
        out_shape=[
            jax.ShapeDtypeStruct((OPS, 2, count, count), F32),
            jax.ShapeDtypeStruct((tiles // pair, 3 * pair, 2 * count, LANES), BF16),
            jax.ShapeDtypeStruct((1, LANES), jnp.int32),
        ],
        scratch_shapes=[
            VMEM((steps, 3 * pair, 2 * count, LANES), BF16),
            VMEM((2, 3 * pair, 6 * count, LANES), BF16),
            VMEM((6 * count, 2 * count), F32),
            VMEM((planes, 2 * count, 2 * count), F32),
            VMEM((GROUP * spots, GROUP * spots), BF16),
        ],
        compiler_params=limit(26),
        cost_estimate=cost(8 * 10**9, 5 * 10**6),
        name="gram",
    )(low, high, u, phases, *tables)


def edge_kernel(count, rows, cores, low_ref, high_ref, lhs_ref, sums_ref, keep_ref, send_ref, tot_ref):
    total = None
    for half in range(low_ref.shape[0]):
        sides = [joined([ref[half, k] for k in range(ref.shape[1])]) for ref in (low_ref, high_ref, lhs_ref)]
        got = nt_dot(jnp.concatenate(sides[:2], axis=0), sides[2])
        total = got if total is None else total + got
    reals, imags = [], []
    at = 0
    for size in (lead_count(count), count - lead_count(count)):
        mid, end = at + size, at + 2 * size
        reals.append(total[at:mid, :count] + total[mid:end, count:])
        imags.append(total[at:mid, count:] - total[mid:end, :count])
        at = end
    real, imag = jnp.concatenate(reals, axis=0), jnp.concatenate(imags, axis=0)
    tot_ref[0] = 0.5 * (real - real.T)
    tot_ref[1] = 0.5 * (imag + imag.T)
    mine = lax.axis_index("space") & (cores - 1)
    for chip in range(count // (rows * cores)):
        for which, ref in ((mine, keep_ref), (1 - mine, send_ref)):
            at = pl.multiple_of((chip * cores + which) * rows, rows)
            for op in range(OPS):
                for half in range(2):
                    piece = sums_ref[op, half, pl.ds(at, rows), :]
                    if op == 1:
                        piece = piece + tot_ref[half, pl.ds(at, rows), :]
                    ref[chip, op, half] = piece


def edge(halos, rim_lhs, sums, count, rows, cores):
    shape = jax.ShapeDtypeStruct((count // (rows * cores), OPS, 2, rows, count), F32)
    return pl.pallas_call(
        partial(edge_kernel, count, rows, cores),
        in_specs=[vspec()] * 4,
        out_specs=[vspec(), vspec()],
        out_shape=[shape, shape],
        scratch_shapes=[VMEM((2, count, count), F32)],
        compiler_params=limit(8),
        cost_estimate=cost(10**9, 3 * 10**6),
        name="edge",
    )(*halos, rim_lhs, sums)


def split_sum(block):
    high = block[0:1].astype(BF16)
    low = (block[0:1] - high.astype(F32)).astype(BF16)
    return jnp.concatenate([high, low, block[1:].astype(BF16)], axis=0)


def fold_kernel(chips, cores, keep_ref, got_ref, own_ref, *out_refs):
    me = lax.axis_index("space") // cores
    own_ref[...] = keep_ref[me] + got_ref[me]
    for step in range(1, chips):
        to = me ^ step
        out_refs[step - 1][...] = split_sum(keep_ref[to] + got_ref[to])


def fold(keep, got, cores):
    chips = keep.shape[0]
    shape = keep.shape[1:]
    sent = jax.ShapeDtypeStruct((shape[0] + 1,) + shape[1:], BF16)
    return pl.pallas_call(
        partial(fold_kernel, chips, cores),
        in_specs=[vspec()] * 2,
        out_specs=[vspec()] * chips,
        out_shape=[jax.ShapeDtypeStruct(shape, F32)] + [sent] * (chips - 1),
        compiler_params=limit(4),
        cost_estimate=cost(10**6, 10**6),
        name="fold",
    )(keep, got)


def total_kernel(own_ref, *refs):
    total_ref = refs[-1]
    first = own_ref[0:1]
    rest = own_ref[1:]
    for ref in refs[:-1]:
        first = first + (ref[0:1].astype(F32) + ref[1:2].astype(F32))
        rest = rest + ref[2:].astype(F32)
    total_ref[0:1] = first.astype(BF16)
    total_ref[1:] = rest.astype(BF16)


def total_rows(parts):
    return pl.pallas_call(
        total_kernel,
        in_specs=[vspec()] * len(parts),
        out_specs=vspec(),
        out_shape=jax.ShapeDtypeStruct(parts[0].shape, BF16),
        compiler_params=limit(4),
        cost_estimate=cost(10**6, 10**6),
        name="total",
    )(*parts)


def dress_kernel(groups, slots, taus, rows, count, table_any, per_ref, *refs):
    slab_refs = refs[:groups]
    out_hbm, lhs_ref, prod_ref, stage_ref, table_ref, sems = refs[groups:]
    table_copy = pltpu.make_async_copy(table_any, table_ref, sems.at[groups])
    table_copy.start()
    me = lax.axis_index("tm")
    for step in range(groups):
        group = me ^ step
        for op in range(OPS):
            at = pl.multiple_of((group * OPS + op) * rows, rows)
            lhs_ref[pl.ds(at, rows), 0:count] = slab_refs[step][op, 0]
            lhs_ref[pl.ds(at, rows), count : 2 * count] = slab_refs[step][op, 1]
    left = lhs_ref[...]
    for tau in range(taus):
        real, imag = per_ref[tau, 0], per_ref[tau, 1]
        right = jnp.concatenate([joined([real, imag]), joined([-imag, real])], axis=0)
        got = jnp.dot(left, right, preferred_element_type=F32).astype(BF16)
        for piece in range(groups * OPS):
            for half in range(2):
                prod_ref[tau * groups * OPS + piece, half] = got[
                    piece * rows : (piece + 1) * rows, half * count : (half + 1) * count
                ]
    prod_ref[taus * groups * OPS] = jnp.zeros((2, rows, count), BF16)
    table_copy.wait()
    copies = []
    for group in range(groups):
        for slot in range(slots):
            stage_ref[group, slot] = prod_ref[table_ref[0, group * slots + slot]]
        copies.append(pltpu.make_async_copy(stage_ref.at[group], out_hbm.at[group], sems.at[group]))
        copies[group].start()
    for copy in copies:
        copy.wait()


def dress(table, per, slabs, groups, slots, rows, count):
    taus = per.shape[0]
    shape = (groups, slots, 2, rows, count)
    return pl.pallas_call(
        partial(dress_kernel, groups, slots, taus, rows, count),
        in_specs=[pl.BlockSpec(memory_space=pl.ANY), vspec()] + [vspec()] * groups,
        out_specs=pl.BlockSpec(memory_space=pltpu.HBM),
        out_shape=jax.ShapeDtypeStruct(shape, BF16),
        scratch_shapes=[
            VMEM((groups * OPS * rows, 2 * count), BF16),
            VMEM((taus * groups * OPS + 1, 2, rows, count), BF16),
            VMEM(shape, BF16),
            SMEM(table.shape, jnp.int32),
            pltpu.SemaphoreType.DMA((groups + 1,)),
        ],
        compiler_params=limit(8),
        cost_estimate=cost(10**9, 2 * 10**6),
        name="dress",
    )(table, per, *slabs)


def fast_shards(eigvecs, gauge_links, perambulator, job_owner, job_elemental, job_source, job_spin):
    count = eigvecs.shape[1]
    planes, sites = eigvecs.shape[4], eigvecs.shape[5]
    tiles = sites // LANES
    space_size = lax.axis_size("space")
    groups = lax.axis_size("tm")
    lx = planes * space_size
    rows = count // space_size
    slots = 3 * ((JOB_DEV + groups - 1) // groups)
    cores = 2

    def tiled(field):
        head = field.shape[:-2]
        order = tuple(range(len(head))) + (len(head) + 1, len(head), len(head) + 2)
        split = field.reshape(head + (planes, tiles, LANES))
        return split.transpose(order).reshape(-1, LANES)

    x = tiled(eigvecs)
    u = tiled(gauge_links)
    angle = 2.0 * math.pi / lx * np.arange(lx)
    phases = jnp.asarray(np.concatenate([np.cos(angle), np.sin(angle)]).astype(np.float32)[None])

    per = perambulator.reshape(-1, 2, count, count)
    empty = per.shape[0] * groups * OPS
    x = pltpu.with_memory_space_constraint(x, pltpu.HBM)
    u = pltpu.with_memory_space_constraint(u, pltpu.HBM)
    up = [(i, (i + 1) % space_size) for i in range(space_size)]
    rim, low, links = rim_plane(x, u, None, count, tiles, planes)
    halos = [lax.ppermute(rim, "space", up)]
    rim, high, u = rim_plane(x, u, links, count, tiles, planes)
    halos.append(lax.ppermute(rim, "space", up))
    tables = [job.reshape(1, -1) for job in (job_owner, job_elemental, job_source, job_spin)]
    sums, rim_lhs, table = gram(
        low, high, u, phases, tables, count, tiles, planes, lx, groups, slots, empty
    )
    keep, send = edge(halos, rim_lhs, sums, count, rows, cores)
    got = lax.ppermute(send, "space", [(i, i ^ 1) for i in range(space_size)])
    parts = fold(keep, got, cores)
    summed = [parts[0]]
    chips = space_size // cores
    for step in range(1, chips):
        summed.append(
            lax.ppermute(parts[step], "space", [(i, i ^ (step * cores)) for i in range(space_size)])
        )
    own = total_rows(summed)
    slabs = [own]
    for step in range(1, groups):
        slabs.append(lax.ppermute(own, "tm", [(i, i ^ step) for i in range(groups)]))
    return dress(table, per, slabs, groups, slots, rows, count)[None]


def passed_along(shard, axis, by):
    count = lax.axis_size(axis)
    return lax.ppermute(shard, axis, [(i, (i + by) % count) for i in range(count)])


def shifted_sites(lattice_field, direction, offset):
    shaped = lattice_field.reshape(lattice_field.shape[:-1] + (LY, LZ))
    rolled = jnp.roll(shaped, -offset, axis=direction - 4)
    return rolled.reshape(lattice_field.shape)


def apply_link(link_field, vectors):
    total_re = None
    total_im = None
    for colour in range(3):
        link_re = link_field[0, :, colour][None]
        link_im = link_field[1, :, colour][None]
        vector_re = vectors[:, 0, colour][:, None]
        vector_im = vectors[:, 1, colour][:, None]
        part_re = link_re * vector_re - link_im * vector_im
        part_im = link_re * vector_im + link_im * vector_re
        if colour == 0:
            total_re, total_im = (part_re, part_im)
        else:
            total_re = total_re + part_re
            total_im = total_im + part_im
    return jnp.stack([total_re, total_im], axis=1)


def stacked_form(vectors):
    vector_count = vectors.shape[0]
    swapped = jnp.concatenate([-vectors[:, 1:2], vectors[:, 0:1]], axis=1)
    return jnp.concatenate(
        [vectors.reshape(vector_count, -1), swapped.reshape(vector_count, -1)], axis=0
    )


def paired_gram(stacked, lattice_field):
    vector_count = lattice_field.shape[0]
    flat_field = lattice_field.astype(jnp.bfloat16).reshape(vector_count, -1)
    product = lax.dot_general(
        stacked, flat_field, (((1,), (1,)), ((), ())), preferred_element_type=jnp.float32
    )
    return product.reshape(2, vector_count, vector_count)


def twisted_field(vectors, xcoord):
    phase_angle = 2.0 * math.pi / (vectors.shape[3] * lax.axis_size("space")) * xcoord
    cosine = jnp.cos(phase_angle)[:, None]
    sine_part = jnp.sin(phase_angle)[:, None]
    real_part = cosine * vectors[:, 0] + sine_part * vectors[:, 1]
    imag_part = cosine * vectors[:, 1] - sine_part * vectors[:, 0]
    return jnp.stack([real_part, imag_part], axis=1)


def antihermitian(paired):
    return 0.5 * jnp.stack([paired[0] - paired[0].T, paired[1] + paired[1].T], axis=0)


def plain_shards(eigvecs, gauge_links, perambulator, job_owner, job_elemental, job_source, job_spin):
    slice_count = eigvecs.shape[0]
    vector_count = eigvecs.shape[1]
    planes = eigvecs.shape[4]
    space_size = lax.axis_size("space")
    group_count = lax.axis_size("tm")
    row_count = vector_count // space_size
    capacity = 3 * ((JOB_DEV + group_count - 1) // group_count)
    xcoord = (lax.axis_index("space") * planes + jnp.arange(planes, dtype=jnp.int32)).astype(
        jnp.float32
    )
    upper_plane = passed_along(eigvecs[:, :, :, :, 0:1], "space", -1)
    low_vectors = eigvecs[0]
    vectors = low_vectors.astype(jnp.float32)
    stacked = stacked_form(low_vectors)
    results = [paired_gram(stacked, twisted_field(vectors, xcoord))]
    for direction in (1, 2, 3):
        link_field = gauge_links[0, direction - 1]
        if direction == 1:
            upper_rim = upper_plane[0].astype(jnp.float32)
            above_field = jnp.concatenate([vectors[:, :, :, 1:], upper_rim], axis=3)
        else:
            above_field = shifted_sites(vectors, direction, 1)
        forward = apply_link(link_field, above_field)
        results.append(antihermitian(paired_gram(stacked, forward)))
    partial_list = [jnp.stack(results, axis=0)]
    partial_value = jnp.stack(partial_list, axis=0)
    summed = lax.psum(partial_value, "space")
    own_rows = lax.dynamic_slice_in_dim(summed, lax.axis_index("space") * row_count, row_count, 3)
    slab_table = own_rows.astype(jnp.bfloat16).reshape(
        slice_count * OPS, 2 * row_count * vector_count
    )
    owners = job_owner[:, 0].reshape(group_count, -1)
    elements = job_elemental.reshape(group_count, -1)
    position = jnp.arange(owners.shape[1], dtype=jnp.int32)
    earlier = position[None, :] < position[:, None]
    same_owner = owners[:, :, None] == owners[:, None, :]
    slot_rank = jnp.sum(jnp.where(same_owner & earlier[None], 1, 0), axis=2).astype(jnp.int32)
    own_group = lax.axis_index("tm")
    slot_count = group_count * capacity
    live_jobs = owners == own_group
    slot_match = live_jobs[:, None, :] & (
        slot_rank[:, None, :] == jnp.arange(capacity, dtype=jnp.int32)[None, :, None]
    )
    sender_owners = lax.dynamic_index_in_dim(owners, own_group, 0, keepdims=False)
    sender_ranks = lax.dynamic_index_in_dim(slot_rank, own_group, 0, keepdims=False)
    sender_elements = lax.dynamic_index_in_dim(elements, own_group, 0, keepdims=False)
    slot_ids = sender_owners * capacity + sender_ranks
    slot_hot = (jnp.arange(slot_count, dtype=jnp.int32)[:, None] == slot_ids[None, :]).astype(
        jnp.float32
    )
    elem_hot = (
        sender_elements[:, None] == jnp.arange(slice_count * OPS, dtype=jnp.int32)[None, :]
    ).astype(jnp.float32)
    picker = jnp.dot(slot_hot, elem_hot, precision=lax.Precision.HIGHEST).astype(jnp.bfloat16)
    outgoing = jnp.dot(picker, slab_table, preferred_element_type=jnp.float32).astype(jnp.bfloat16)
    outgoing = outgoing.reshape(group_count, capacity, 2, row_count, vector_count)
    received = lax.all_to_all(outgoing, "tm", split_axis=0, concat_axis=0, tiled=True)
    block_index = job_source.reshape(group_count, -1) * SPIN + job_spin.reshape(group_count, -1)
    tau_index = jnp.sum(jnp.where(slot_match, block_index[:, None, :], 0), axis=2)
    blocks = perambulator.reshape(-1, 2 * vector_count, vector_count)
    chosen = jnp.take(blocks, tau_index.reshape(-1), axis=0)
    slab_rows = received.reshape(slot_count, 2, row_count, vector_count)
    real_rows = jnp.concatenate([slab_rows[:, 0], -slab_rows[:, 1]], axis=-1)
    imag_rows = jnp.concatenate([slab_rows[:, 1], slab_rows[:, 0]], axis=-1)
    left_side = jnp.stack([real_rows, imag_rows], axis=1).reshape(
        slot_count, 2 * row_count, 2 * vector_count
    )
    dressed = lax.dot_general(
        left_side, chosen, (((2,), (1,)), ((0,), (0,))), preferred_element_type=jnp.float32
    )
    return dressed.astype(jnp.bfloat16).reshape(
        1, group_count, capacity, 2, row_count, vector_count
    )


def shards(*args):
    eigvecs = args[0]
    count, planes, sites = eigvecs.shape[1], eigvecs.shape[4], eigvecs.shape[5]
    space_size, groups = lax.axis_size("space"), lax.axis_size("tm")
    whole_tiles = sites % (2 * LANES) == 0 and count == LANES and planes * (sites // LANES) == GROUP
    fits = groups * 3 * ((JOB_DEV + groups - 1) // groups) < LANES
    powers = space_size & (space_size - 1) == 0 and groups & (groups - 1) == 0
    small = space_size * GROUP == count and groups <= 8 and args[3].shape[0] <= LANES
    if whole_tiles and fits and powers and small and eigvecs.shape[0] == 1:
        return fast_shards(*args)
    return plain_shards(*args)


def solution(mesh):
    return jax.shard_map(
        shards,
        mesh=mesh,
        in_specs=(
            P("tm", None, None, None, "space", None),
            P("tm", None, None, None, None, "space", None),
            P("tm", None, None, None, None),
            P(),
            P(),
            P(),
            P(),
        ),
        out_specs=P("tm", None, None, None, "space", None),
        check_vma=False,
    )
```

profile of v0, /device:TPU:0, one launch (start us, length us, event | category | flops | bytes accessed | tf_op | source)
XLA Modules:
  0.0 35.1 jit_solution(10716202716089010380)
XLA Ops:
  0.0 0.0 copy-start.1
  0.0 0.0 copy-start.2
  0.0 1.6 %rim.1 = (bf16[2,6,64,128]{3,2,1,0:T(8,128)(2,1)S(1)}, bf16[3072,128]{1,0:T(8,128)(2,1)S(1)}, f32[4,27,8,128]{3,2,1,0:T(8,128)S(1)}) custom-call(bf16[12288,128]{1,0:T(8,128)(2,1)} %bitcast.21, f32[864,128]{1,0:T(8,128)} %bitcast.23), custom_call_target="tpu_custom_call" | custom-call | flops 100000000 | bytes 2000000 | tf_op jit(solution)/shard_map/rim/pallas_call | solution.py:130
  1.6 0.5 %collective-permute-start = (bf16[2,6,64,128]{3,2,1,0:T(8,128)(2,1)S(1)}, bf16[2,6,64,128]{3,2,1,0:T(8,128)(2,1)S(1)}, u32[]{:S(2)}, u32[]{:S(2)}) collective-permute-start(bf16[2,6,64,128]{3,2,1,0:T(8,128)(2,1)S(1)} %get-tuple-element.25), channel_id=1, source_target_pairs={{0,1},{1,2},{2,3},{3,4},{4,5},{5,6},{6,7},{7,0},{8,9},{9,10},{10,1... | collective-permute-start | bytes 589832 | tf_op jit(solution)/shard_map/ppermute | solution.py:583
  2.2 2.5 %rest.1 = (bf16[2,6,192,128]{3,2,1,0:T(8,128)(2,1)S(1)}, bf16[9216,128]{1,0:T(8,128)(2,1)S(1)}, f32[864,128]{1,0:T(8,128)S(1)}) custom-call(bf16[12288,128]{1,0:T(8,128)(2,1)} %bitcast.22, f32[864,128]{1,0:T(8,128)} %bitcast.24, f32[4,27,8,128]{3,2,1,0:T(8,128)S(1)} %get-tuple-element.21.refs_0_), custom_call_target="tpu_custom_call" | custom-call | flops 100000000 | bytes 2000000 | tf_op jit(solution)/shard_map/rest/pallas_call | solution.py:130
  4.7 2.6 %collective-permute-start.1 = (bf16[2,6,192,128]{3,2,1,0:T(8,128)(2,1)S(1)}, bf16[2,6,192,128]{3,2,1,0:T(8,128)(2,1)S(1)}, u32[]{:S(2)}, u32[]{:S(2)}) collective-permute-start(bf16[2,6,192,128]{3,2,1,0:T(8,128)(2,1)S(1)} %get-tuple-element.26), channel_id=1, source_target_pairs={{0,1},{1,2},{2,3},{3,4},{4,5},{5,6},{6,7},{7,0},{8,9},{9,10},{10,1... | collective-permute-start | bytes 1769480 | tf_op jit(solution)/shard_map/ppermute | solution.py:585
  7.3 0.0 copy-done.1
  7.3 0.0 copy-done.2
  7.3 0.0 copy-done.3
  7.3 0.0 copy-done.4
  7.3 0.0 copy-done.5
  7.3 7.9 %gram.1 = (f32[4,2,128,128]{3,2,1,0:T(8,128)S(1)}, bf16[2,6,256,128]{3,2,1,0:T(8,128)(2,1)S(1)}, s32[1,128]{1,0:T(1,128)S(1)}) custom-call(bf16[3072,128]{1,0:T(8,128)(2,1)S(1)} %get-tuple-element.20.low_ref, bf16[9216,128]{1,0:T(8,128)(2,1)S(1)} %get-tuple-element.22.high_ref, f32[864,128]{1,0:T(8,128)S(1)} %get-tuple-element.23.u_ref, ...), custom_call_target="tpu_custom_call" | custom-call | flops 8000000000 | bytes 5000000 | tf_op jit(solution)/shard_map/gram/pallas_call | solution.py:384
  15.2 0.0 copy-start
  15.2 0.0 collective-permute-done.low_ref
  15.2 0.0 collective-permute-done.1.high_ref
  15.2 0.5 %edge.1 = (f32[4,4,2,16,128]{4,3,2,1,0:T(8,128)S(1)}, f32[4,4,2,16,128]{4,3,2,1,0:T(8,128)S(1)}) custom-call(bf16[2,6,64,128]{3,2,1,0:T(8,128)(2,1)S(1)} %collective-permute-done.low_ref, bf16[2,6,192,128]{3,2,1,0:T(8,128)(2,1)S(1)} %collective-permute-done.1.high_ref, bf16[2,6,256,128]{3,2,1,0:T(8,128)(2,1)S(1)} %get-tuple-element.27.lhs_ref, ...), custom_call_target="tpu_custom_call" | custom-call | flops 1000000000 | bytes 3000000 | tf_op jit(solution)/shard_map/edge/pallas_call | solution.py:436
  15.7 0.1 collective-permute-start.2
  15.8 1.5 %collective-permute-done.2.got_ref = f32[4,4,2,16,128]{4,3,2,1,0:T(8,128)S(1)} collective-permute-done((f32[4,4,2,16,128]{4,3,2,1,0:T(8,128)S(1)}, f32[4,4,2,16,128]{4,3,2,1,0:T(8,128)S(1)}, u32[]{:S(2)}, u32[]{:S(2)}) %collective-permute-start.2) | collective-permute-done | bytes 262176 | tf_op jit(solution)/shard_map/ppermute | solution.py:591
  17.4 1.6 %collective-permute-start.3 = (bf16[5,2,16,128]{3,2,1,0:T(8,128)(2,1)S(1)}, bf16[5,2,16,128]{3,2,1,0:T(8,128)(2,1)S(1)}, u32[]{:S(2)}, u32[]{:S(2)}) collective-permute-start(bf16[5,2,16,128]{3,2,1,0:T(8,128)(2,1)S(1)} %get-tuple-element.32), channel_id=1, source_target_pairs={{0,2},{1,3},{2,0},{3,1},{4,6},{5,7},{6,4},{7,5},{8,10},{9,11},{10,... | collective-permute-start | bytes 122888 | tf_op jit(solution)/shard_map/ppermute | solution.py:597
  18.9 1.3 %collective-permute-start.4 = (bf16[5,2,16,128]{3,2,1,0:T(8,128)(2,1)S(1)}, bf16[5,2,16,128]{3,2,1,0:T(8,128)(2,1)S(1)}, u32[]{:S(2)}, u32[]{:S(2)}) collective-permute-start(bf16[5,2,16,128]{3,2,1,0:T(8,128)(2,1)S(1)} %get-tuple-element.33), channel_id=1, source_target_pairs={{0,4},{1,5},{2,6},{3,7},{4,0},{5,1},{6,2},{7,3},{8,12},{9,13},{10,... | collective-permute-start | bytes 122888 | tf_op jit(solution)/shard_map/ppermute | solution.py:597
  20.2 0.9 %collective-permute-start.5 = (bf16[5,2,16,128]{3,2,1,0:T(8,128)(2,1)S(1)}, bf16[5,2,16,128]{3,2,1,0:T(8,128)(2,1)S(1)}, u32[]{:S(2)}, u32[]{:S(2)}) collective-permute-start(bf16[5,2,16,128]{3,2,1,0:T(8,128)(2,1)S(1)} %get-tuple-element.34), channel_id=1, source_target_pairs={{0,6},{1,7},{2,4},{3,5},{4,2},{5,3},{6,0},{7,1},{8,14},{9,15},{10,... | collective-permute-start | bytes 122888 | tf_op jit(solution)/shard_map/ppermute | solution.py:597
  21.1 0.3 collective-permute-done.3.refs_0_
  21.4 1.5 %collective-permute-done.4.refs_1_ = bf16[5,2,16,128]{3,2,1,0:T(8,128)(2,1)S(1)} collective-permute-done((bf16[5,2,16,128]{3,2,1,0:T(8,128)(2,1)S(1)}, bf16[5,2,16,128]{3,2,1,0:T(8,128)(2,1)S(1)}, u32[]{:S(2)}, u32[]{:S(2)}) %collective-permute-start.4) | collective-permute-done | bytes 40992 | tf_op jit(solution)/shard_map/ppermute | solution.py:597
  22.9 2.2 %collective-permute-done.5.refs_2_ = bf16[5,2,16,128]{3,2,1,0:T(8,128)(2,1)S(1)} collective-permute-done((bf16[5,2,16,128]{3,2,1,0:T(8,128)(2,1)S(1)}, bf16[5,2,16,128]{3,2,1,0:T(8,128)(2,1)S(1)}, u32[]{:S(2)}, u32[]{:S(2)}) %collective-permute-start.5) | collective-permute-done | bytes 40992 | tf_op jit(solution)/shard_map/ppermute | solution.py:597
  25.2 3.7 %collective-permute-start.8 = (bf16[4,2,16,128]{3,2,1,0:T(8,128)(2,1)S(1)}, bf16[4,2,16,128]{3,2,1,0:T(8,128)(2,1)S(1)}, u32[]{:S(2)}, u32[]{:S(2)}) collective-permute-start(bf16[4,2,16,128]{3,2,1,0:T(8,128)(2,1)S(1)} %total.1.refs_0_), channel_id=1, source_target_pairs={{0,24},{8,16},{16,8},{24,0},{1,25},{9,17},{17,9},{25,1},{2,26},{10... | collective-permute-start | bytes 98312 | tf_op jit(solution)/shard_map/ppermute | solution.py:602
  28.8 0.0 collective-permute-start.7
  28.8 0.8 %collective-permute-start.6 = (bf16[4,2,16,128]{3,2,1,0:T(8,128)(2,1)S(1)}, bf16[4,2,16,128]{3,2,1,0:T(8,128)(2,1)S(1)}, u32[]{:S(2)}, u32[]{:S(2)}) collective-permute-start(bf16[4,2,16,128]{3,2,1,0:T(8,128)(2,1)S(1)} %total.1.refs_0_), channel_id=1, source_target_pairs={{0,8},{8,0},{16,24},{24,16},{1,9},{9,1},{17,25},{25,17},{2,10},{10... | collective-permute-start | bytes 98312 | tf_op jit(solution)/shard_map/ppermute | solution.py:602
  29.6 1.4 %collective-permute-done.8.refs_3_ = bf16[4,2,16,128]{3,2,1,0:T(8,128)(2,1)S(1)} collective-permute-done((bf16[4,2,16,128]{3,2,1,0:T(8,128)(2,1)S(1)}, bf16[4,2,16,128]{3,2,1,0:T(8,128)(2,1)S(1)}, u32[]{:S(2)}, u32[]{:S(2)}) %collective-permute-start.8) | collective-permute-done | bytes 32800 | tf_op jit(solution)/shard_map/ppermute | solution.py:602
  31.0 2.6 %collective-permute-done.7.refs_2_ = bf16[4,2,16,128]{3,2,1,0:T(8,128)(2,1)S(1)} collective-permute-done((bf16[4,2,16,128]{3,2,1,0:T(8,128)(2,1)S(1)}, bf16[4,2,16,128]{3,2,1,0:T(8,128)(2,1)S(1)}, u32[]{:S(2)}, u32[]{:S(2)}) %collective-permute-start.7) | collective-permute-done | bytes 32800 | tf_op jit(solution)/shard_map/ppermute | solution.py:602
  33.6 0.0 collective-permute-done.6.refs_1_
  33.6 0.0 copy-done
  33.6 1.5 %dress.1 = bf16[4,18,2,16,128]{4,3,2,1,0:T(8,128)(2,1)} custom-call(s32[1,128]{1,0:T(1,128)S(1)} %get-tuple-element.24.table_any, bf16[8,2,128,128]{3,2,1,0:T(8,128)(2,1)S(1)} %bitcast.16, bf16[4,2,16,128]{3,2,1,0:T(8,128)(2,1)S(1)} %total.1.refs_0_, bf16[4,2,16,128]{3,2,1,0:T(8,128)(2,1)S(1)} %collective-permute-done.6.refs_1_, ...), custom_call_target="tpu_custom_call" | custom-call | flops 1000000000 | bytes 2000000 | tf_op jit(solution)/shard_map/dress/pallas_call | solution.py:537
  (5 shorter events, 0.1 us)
Async XLA Ops:
  0.0 7.3 %copy-start.1 = (s32[96,1]{0,1:T(1,128)S(1)}, s32[96,1]{0,1:T(1,128)}, u32[]{:S(2)}) copy-start(s32[96,1]{0,1:T(1,128)} %param.11) | copy-start | bytes 1156
  0.0 7.3 %copy-start.2 = (s32[96]{0:T(128)S(1)}, s32[96]{0:T(128)}, u32[]{:S(2)}) copy-start(s32[96]{0:T(128)} %param.12) | copy-start | bytes 1156
  0.0 7.3 %copy-start.3 = (s32[96]{0:T(128)S(1)}, s32[96]{0:T(128)}, u32[]{:S(2)}) copy-start(s32[96]{0:T(128)} %param.13) | copy-start | bytes 1156
  0.0 7.3 %copy-start.4 = (s32[96]{0:T(128)S(1)}, s32[96]{0:T(128)}, u32[]{:S(2)}) copy-start(s32[96]{0:T(128)} %param.14) | copy-start | bytes 1156
  0.0 7.3 %copy-start.5 = (f32[1,64]{1,0:T(1,128)S(1)}, f32[1,64]{1,0:T(1,128)}, u32[]{:S(2)}) copy-start(f32[1,64]{1,0:T(1,128)} %constant.2.clone.phase_ref) | copy-start | bytes 772
  1.6 13.6 %collective-permute-start = (bf16[2,6,64,128]{3,2,1,0:T(8,128)(2,1)S(1)}, bf16[2,6,64,128]{3,2,1,0:T(8,128)(2,1)S(1)}, u32[]{:S(2)}, u32[]{:S(2)}) collective-permute-start(bf16[2,6,64,128]{3,2,1,0:T(8,128)(2,1)S(1)} %get-tuple-element.25), channel_id=1, source_target_pairs={{0,1},{1,2},{2,3},{3,4},{4,5},{5,6},{6,7},{7,0},{8,9},{9,10},{10,1... | collective-permute-start | bytes 589832 | tf_op jit(solution)/shard_map/ppermute | solution.py:583
  4.7 10.6 %collective-permute-start.1 = (bf16[2,6,192,128]{3,2,1,0:T(8,128)(2,1)S(1)}, bf16[2,6,192,128]{3,2,1,0:T(8,128)(2,1)S(1)}, u32[]{:S(2)}, u32[]{:S(2)}) collective-permute-start(bf16[2,6,192,128]{3,2,1,0:T(8,128)(2,1)S(1)} %get-tuple-element.26), channel_id=1, source_target_pairs={{0,1},{1,2},{2,3},{3,4},{4,5},{5,6},{6,7},{7,0},{8,9},{9,10},{10,1... | collective-permute-start | bytes 1769480 | tf_op jit(solution)/shard_map/ppermute | solution.py:585
  15.2 18.4 %copy-start = (bf16[2,4,2,128,128]{4,3,2,1,0:T(8,128)(2,1)S(1)}, bf16[2,4,2,128,128]{4,3,2,1,0:T(8,128)(2,1)}, u32[]{:S(2)}) copy-start(bf16[2,4,2,128,128]{4,3,2,1,0:T(8,128)(2,1)} %param.10) | copy-start | bytes 1572868
  15.7 1.6 %collective-permute-start.2 = (f32[4,4,2,16,128]{4,3,2,1,0:T(8,128)S(1)}, f32[4,4,2,16,128]{4,3,2,1,0:T(8,128)S(1)}, u32[]{:S(2)}, u32[]{:S(2)}) collective-permute-start(f32[4,4,2,16,128]{4,3,2,1,0:T(8,128)S(1)} %get-tuple-element.30), channel_id=1, source_target_pairs={{0,1},{1,0},{2,3},{3,2},{4,5},{5,4},{6,7},{7,6},{8,9},{9,8},{10,11... | collective-permute-start | bytes 786440 | tf_op jit(solution)/shard_map/ppermute | solution.py:591
  17.4 4.1 %collective-permute-start.3 = (bf16[5,2,16,128]{3,2,1,0:T(8,128)(2,1)S(1)}, bf16[5,2,16,128]{3,2,1,0:T(8,128)(2,1)S(1)}, u32[]{:S(2)}, u32[]{:S(2)}) collective-permute-start(bf16[5,2,16,128]{3,2,1,0:T(8,128)(2,1)S(1)} %get-tuple-element.32), channel_id=1, source_target_pairs={{0,2},{1,3},{2,0},{3,1},{4,6},{5,7},{6,4},{7,5},{8,10},{9,11},{10,... | collective-permute-start | bytes 122888 | tf_op jit(solution)/shard_map/ppermute | solution.py:597
  18.9 4.0 %collective-permute-start.4 = (bf16[5,2,16,128]{3,2,1,0:T(8,128)(2,1)S(1)}, bf16[5,2,16,128]{3,2,1,0:T(8,128)(2,1)S(1)}, u32[]{:S(2)}, u32[]{:S(2)}) collective-permute-start(bf16[5,2,16,128]{3,2,1,0:T(8,128)(2,1)S(1)} %get-tuple-element.33), channel_id=1, source_target_pairs={{0,4},{1,5},{2,6},{3,7},{4,0},{5,1},{6,2},{7,3},{8,12},{9,13},{10,... | collective-permute-start | bytes 122888 | tf_op jit(solution)/shard_map/ppermute | solution.py:597
  20.2 4.9 %collective-permute-start.5 = (bf16[5,2,16,128]{3,2,1,0:T(8,128)(2,1)S(1)}, bf16[5,2,16,128]{3,2,1,0:T(8,128)(2,1)S(1)}, u32[]{:S(2)}, u32[]{:S(2)}) collective-permute-start(bf16[5,2,16,128]{3,2,1,0:T(8,128)(2,1)S(1)} %get-tuple-element.34), channel_id=1, source_target_pairs={{0,6},{1,7},{2,4},{3,5},{4,2},{5,3},{6,0},{7,1},{8,14},{9,15},{10,... | collective-permute-start | bytes 122888 | tf_op jit(solution)/shard_map/ppermute | solution.py:597
  25.2 5.9 %collective-permute-start.8 = (bf16[4,2,16,128]{3,2,1,0:T(8,128)(2,1)S(1)}, bf16[4,2,16,128]{3,2,1,0:T(8,128)(2,1)S(1)}, u32[]{:S(2)}, u32[]{:S(2)}) collective-permute-start(bf16[4,2,16,128]{3,2,1,0:T(8,128)(2,1)S(1)} %total.1.refs_0_), channel_id=1, source_target_pairs={{0,24},{8,16},{16,8},{24,0},{1,25},{9,17},{17,9},{25,1},{2,26},{10... | collective-permute-start | bytes 98312 | tf_op jit(solution)/shard_map/ppermute | solution.py:602
  28.8 4.8 %collective-permute-start.7 = (bf16[4,2,16,128]{3,2,1,0:T(8,128)(2,1)S(1)}, bf16[4,2,16,128]{3,2,1,0:T(8,128)(2,1)S(1)}, u32[]{:S(2)}, u32[]{:S(2)}) collective-permute-start(bf16[4,2,16,128]{3,2,1,0:T(8,128)(2,1)S(1)} %total.1.refs_0_), channel_id=1, source_target_pairs={{0,16},{8,24},{16,0},{24,8},{1,17},{9,25},{17,1},{25,9},{2,18},{10... | collective-permute-start | bytes 98312 | tf_op jit(solution)/shard_map/ppermute | solution.py:602
  28.8 4.8 %collective-permute-start.6 = (bf16[4,2,16,128]{3,2,1,0:T(8,128)(2,1)S(1)}, bf16[4,2,16,128]{3,2,1,0:T(8,128)(2,1)S(1)}, u32[]{:S(2)}, u32[]{:S(2)}) collective-permute-start(bf16[4,2,16,128]{3,2,1,0:T(8,128)(2,1)S(1)} %total.1.refs_0_), channel_id=1, source_target_pairs={{0,8},{8,0},{16,24},{24,16},{1,9},{9,1},{17,25},{25,17},{2,10},{10... | collective-permute-start | bytes 98312 | tf_op jit(solution)/shard_map/ppermute | solution.py:602
where the time goes:
time: 35.3 us; the launch traced here: 35.1 us
  Pallas kernels  14 us (40%)
  starting transfers between devices  11.5 us (33%)
  waiting for transfers between devices  9.56 us (27%)
    pallas_call x1, Pallas kernels, gram(): pl.pallas_call(partial(gram_kernel, count, tiles, planes, lx, groups, slo...  7.87 us
    ppermute x3, starting transfers between devices, fast_shards(): lax.ppermute(own, 'tm', [(i, i ^ step) for i in range(groups)])  4.45 us
    pallas_call x2, Pallas kernels, rim_plane(): pl.pallas_call(partial(rim_kernel, tiles, planes, 0 if leads else lead_co...  4.09 us
    ppermute x3, waiting for transfers between devices, fast_shards(): lax.ppermute(parts[step], 'space', [(i, i ^ step * cores) for i in range(...  4.03 us
    ppermute x3, waiting for transfers between devices, fast_shards(): lax.ppermute(own, 'tm', [(i, i ^ step) for i in range(groups)])  4.02 us
    ppermute x3, starting transfers between devices, fast_shards(): lax.ppermute(parts[step], 'space', [(i, i ^ step * cores) for i in range(...  3.73 us
    ppermute x1, starting transfers between devices, fast_shards(): halos.append(lax.ppermute(rim, 'space', up))  2.64 us
    ppermute x1, waiting for transfers between devices, fast_shards(): got = lax.ppermute(send, 'space', [(i, i ^ 1) for i in range(space_size)])  1.5 us
  transfers between devices with their start and end apart: 9, of which 6 were waited for; matrix products, arithmetic and copies ran while one was open for 0% of the time, Pallas kernels for 29%

commit v1 on v0

--- a/solution.py
+++ b/solution.py
@@ -104,7 +104,7 @@
 
 
 def lead_count(count):
-    return count // (4 * GROUP) * GROUP
+    return count * 3 // (8 * GROUP) * GROUP
 
 
 def rim_plane(x, u, links, count, tiles, planes):
@@ -597,9 +597,10 @@
             lax.ppermute(parts[step], "space", [(i, i ^ (step * cores)) for i in range(space_size)])
         )
     own = total_rows(summed)
-    slabs = [own]
-    for step in range(1, groups):
-        slabs.append(lax.ppermute(own, "tm", [(i, i ^ step) for i in range(groups)]))
+    moved = {0: own}
+    for step in sorted(range(1, groups), key=lambda step: (step & 1 == 0, step)):
+        moved[step] = lax.ppermute(own, "tm", [(i, i ^ step) for i in range(groups)])
+    slabs = [moved[step] for step in range(groups)]
     return dress(table, per, slabs, groups, slots, rows, count)[None]
 
 

time: 35.3 us -> 35 us (level)
  no operation moved by 1% of the time
where the time goes in v1:
time: 35 us; the launch traced here: 34.8 us
  Pallas kernels  13.9 us (40%)
  starting transfers between devices  11.3 us (32%)
  waiting for transfers between devices  9.48 us (27%)
    pallas_call x1, Pallas kernels, gram(): pl.pallas_call(partial(gram_kernel, count, tiles, planes, lx, groups, slo...  7.86 us
    ppermute x3, starting transfers between devices, fast_shards(): lax.ppermute(own, 'tm', [(i, i ^ step) for i in range(groups)])  4.45 us
    pallas_call x2, Pallas kernels, rim_plane(): pl.pallas_call(partial(rim_kernel, tiles, planes, 0 if leads else lead_co...  4.09 us
    ppermute x3, waiting for transfers between devices, fast_shards(): lax.ppermute(own, 'tm', [(i, i ^ step) for i in range(groups)])  4.03 us
    ppermute x3, waiting for transfers between devices, fast_shards(): lax.ppermute(parts[step], 'space', [(i, i ^ step * cores) for i in range(...  3.95 us
    ppermute x3, starting transfers between devices, fast_shards(): lax.ppermute(parts[step], 'space', [(i, i ^ step * cores) for i in range(...  3.55 us
    ppermute x1, starting transfers between devices, fast_shards(): halos.append(lax.ppermute(rim, 'space', up))  2.64 us
    ppermute x1, waiting for transfers between devices, fast_shards(): got = lax.ppermute(send, 'space', [(i, i ^ 1) for i in range(space_size)])  1.49 us
  transfers between devices with their start and end apart: 9, of which 6 were waited for; matrix products, arithmetic and copies ran while one was open for 0% of the time, Pallas kernels for 29%

profile of v1, /device:TPU:0, one launch (start us, length us, event | category | flops | bytes accessed | tf_op | source)
XLA Modules:
  0.0 34.8 jit_solution(8504700569169068856)
XLA Ops:
  0.0 1.8 %rim.1 = (bf16[2,6,96,128]{3,2,1,0:T(8,128)(2,1)S(1)}, bf16[4608,128]{1,0:T(8,128)(2,1)S(1)}, f32[4,27,8,128]{3,2,1,0:T(8,128)S(1)}) custom-call(bf16[12288,128]{1,0:T(8,128)(2,1)} %bitcast.21, f32[864,128]{1,0:T(8,128)} %bitcast.23), custom_call_target="tpu_custom_call" | custom-call | flops 100000000 | bytes 2000000 | tf_op jit(solution)/shard_map/rim/pallas_call | solution.py:130
  1.8 0.5 %collective-permute-start = (bf16[2,6,96,128]{3,2,1,0:T(8,128)(2,1)S(1)}, bf16[2,6,96,128]{3,2,1,0:T(8,128)(2,1)S(1)}, u32[]{:S(2)}, u32[]{:S(2)}) collective-permute-start(bf16[2,6,96,128]{3,2,1,0:T(8,128)(2,1)S(1)} %get-tuple-element.25), channel_id=1, source_target_pairs={{0,1},{1,2},{2,3},{3,4},{4,5},{5,6},{6,7},{7,0},{8,9},{9,10},{10,1... | collective-permute-start | bytes 884744 | tf_op jit(solution)/shard_map/ppermute | solution.py:583
  2.4 0.0 copy-start.1
  2.4 0.0 copy-start.5
  2.4 2.3 %rest.1 = (bf16[2,6,160,128]{3,2,1,0:T(8,128)(2,1)S(1)}, bf16[7680,128]{1,0:T(8,128)(2,1)S(1)}, f32[864,128]{1,0:T(8,128)S(1)}) custom-call(bf16[12288,128]{1,0:T(8,128)(2,1)} %bitcast.22, f32[864,128]{1,0:T(8,128)} %bitcast.24, f32[4,27,8,128]{3,2,1,0:T(8,128)S(1)} %get-tuple-element.21.refs_0_), custom_call_target="tpu_custom_call" | custom-call | flops 100000000 | bytes 2000000 | tf_op jit(solution)/shard_map/rest/pallas_call | solution.py:130
  4.7 2.6 %collective-permute-start.1 = (bf16[2,6,160,128]{3,2,1,0:T(8,128)(2,1)S(1)}, bf16[2,6,160,128]{3,2,1,0:T(8,128)(2,1)S(1)}, u32[]{:S(2)}, u32[]{:S(2)}) collective-permute-start(bf16[2,6,160,128]{3,2,1,0:T(8,128)(2,1)S(1)} %get-tuple-element.26), channel_id=1, source_target_pairs={{0,1},{1,2},{2,3},{3,4},{4,5},{5,6},{6,7},{7,0},{8,9},{9,10},{10,1... | collective-permute-start | bytes 1474568 | tf_op jit(solution)/shard_map/ppermute | solution.py:585
  7.3 0.0 copy-done.1
  7.3 0.0 copy-done.2
  7.3 0.0 copy-done.3
  7.3 0.0 copy-done.4
  7.3 0.0 copy-done.5
  7.3 7.9 %gram.1 = (f32[4,2,128,128]{3,2,1,0:T(8,128)S(1)}, bf16[2,6,256,128]{3,2,1,0:T(8,128)(2,1)S(1)}, s32[1,128]{1,0:T(1,128)S(1)}) custom-call(bf16[4608,128]{1,0:T(8,128)(2,1)S(1)} %get-tuple-element.20.low_ref, bf16[7680,128]{1,0:T(8,128)(2,1)S(1)} %get-tuple-element.22.high_ref, f32[864,128]{1,0:T(8,128)S(1)} %get-tuple-element.23.u_ref, ...), custom_call_target="tpu_custom_call" | custom-call | flops 8000000000 | bytes 5000000 | tf_op jit(solution)/shard_map/gram/pallas_call | solution.py:384
  15.2 0.0 collective-permute-done.low_ref
  15.2 0.0 collective-permute-done.1.high_ref
  15.2 0.0 copy-start
  15.2 0.5 %edge.1 = (f32[4,4,2,16,128]{4,3,2,1,0:T(8,128)S(1)}, f32[4,4,2,16,128]{4,3,2,1,0:T(8,128)S(1)}) custom-call(bf16[2,6,96,128]{3,2,1,0:T(8,128)(2,1)S(1)} %collective-permute-done.low_ref, bf16[2,6,160,128]{3,2,1,0:T(8,128)(2,1)S(1)} %collective-permute-done.1.high_ref, bf16[2,6,256,128]{3,2,1,0:T(8,128)(2,1)S(1)} %get-tuple-element.27.lhs_ref, ...), custom_call_target="tpu_custom_call" | custom-call | flops 1000000000 | bytes 3000000 | tf_op jit(solution)/shard_map/edge/pallas_call | solution.py:436
  15.7 0.1 collective-permute-start.2
  15.8 1.5 %collective-permute-done.2.got_ref = f32[4,4,2,16,128]{4,3,2,1,0:T(8,128)S(1)} collective-permute-done((f32[4,4,2,16,128]{4,3,2,1,0:T(8,128)S(1)}, f32[4,4,2,16,128]{4,3,2,1,0:T(8,128)S(1)}, u32[]{:S(2)}, u32[]{:S(2)}) %collective-permute-start.2) | collective-permute-done | bytes 262176 | tf_op jit(solution)/shard_map/ppermute | solution.py:591
  17.4 1.6 %collective-permute-start.3 = (bf16[5,2,16,128]{3,2,1,0:T(8,128)(2,1)S(1)}, bf16[5,2,16,128]{3,2,1,0:T(8,128)(2,1)S(1)}, u32[]{:S(2)}, u32[]{:S(2)}) collective-permute-start(bf16[5,2,16,128]{3,2,1,0:T(8,128)(2,1)S(1)} %get-tuple-element.32), channel_id=1, source_target_pairs={{0,2},{1,3},{2,0},{3,1},{4,6},{5,7},{6,4},{7,5},{8,10},{9,11},{10,... | collective-permute-start | bytes 122888 | tf_op jit(solution)/shard_map/ppermute | solution.py:597
  18.9 1.1 %collective-permute-start.4 = (bf16[5,2,16,128]{3,2,1,0:T(8,128)(2,1)S(1)}, bf16[5,2,16,128]{3,2,1,0:T(8,128)(2,1)S(1)}, u32[]{:S(2)}, u32[]{:S(2)}) collective-permute-start(bf16[5,2,16,128]{3,2,1,0:T(8,128)(2,1)S(1)} %get-tuple-element.33), channel_id=1, source_target_pairs={{0,4},{1,5},{2,6},{3,7},{4,0},{5,1},{6,2},{7,3},{8,12},{9,13},{10,... | collective-permute-start | bytes 122888 | tf_op jit(solution)/shard_map/ppermute | solution.py:597
  20.0 0.9 %collective-permute-start.5 = (bf16[5,2,16,128]{3,2,1,0:T(8,128)(2,1)S(1)}, bf16[5,2,16,128]{3,2,1,0:T(8,128)(2,1)S(1)}, u32[]{:S(2)}, u32[]{:S(2)}) collective-permute-start(bf16[5,2,16,128]{3,2,1,0:T(8,128)(2,1)S(1)} %get-tuple-element.34), channel_id=1, source_target_pairs={{0,6},{1,7},{2,4},{3,5},{4,2},{5,3},{6,0},{7,1},{8,14},{9,15},{10,... | collective-permute-start | bytes 122888 | tf_op jit(solution)/shard_map/ppermute | solution.py:597
  20.9 0.5 %collective-permute-done.3.refs_0_ = bf16[5,2,16,128]{3,2,1,0:T(8,128)(2,1)S(1)} collective-permute-done((bf16[5,2,16,128]{3,2,1,0:T(8,128)(2,1)S(1)}, bf16[5,2,16,128]{3,2,1,0:T(8,128)(2,1)S(1)}, u32[]{:S(2)}, u32[]{:S(2)}) %collective-permute-start.3) | collective-permute-done | bytes 40992 | tf_op jit(solution)/shard_map/ppermute | solution.py:597
  21.4 1.5 %collective-permute-done.4.refs_1_ = bf16[5,2,16,128]{3,2,1,0:T(8,128)(2,1)S(1)} collective-permute-done((bf16[5,2,16,128]{3,2,1,0:T(8,128)(2,1)S(1)}, bf16[5,2,16,128]{3,2,1,0:T(8,128)(2,1)S(1)}, u32[]{:S(2)}, u32[]{:S(2)}) %collective-permute-start.4) | collective-permute-done | bytes 40992 | tf_op jit(solution)/shard_map/ppermute | solution.py:597
  22.9 1.9 %collective-permute-done.5.refs_2_ = bf16[5,2,16,128]{3,2,1,0:T(8,128)(2,1)S(1)} collective-permute-done((bf16[5,2,16,128]{3,2,1,0:T(8,128)(2,1)S(1)}, bf16[5,2,16,128]{3,2,1,0:T(8,128)(2,1)S(1)}, u32[]{:S(2)}, u32[]{:S(2)}) %collective-permute-start.5) | collective-permute-done | bytes 40992 | tf_op jit(solution)/shard_map/ppermute | solution.py:597
  24.9 3.7 %collective-permute-start.8 = (bf16[4,2,16,128]{3,2,1,0:T(8,128)(2,1)S(1)}, bf16[4,2,16,128]{3,2,1,0:T(8,128)(2,1)S(1)}, u32[]{:S(2)}, u32[]{:S(2)}) collective-permute-start(bf16[4,2,16,128]{3,2,1,0:T(8,128)(2,1)S(1)} %total.1.refs_0_), channel_id=1, source_target_pairs={{0,24},{8,16},{16,8},{24,0},{1,25},{9,17},{17,9},{25,1},{2,26},{10... | collective-permute-start | bytes 98312 | tf_op jit(solution)/shard_map/ppermute | solution.py:602
  28.6 0.0 collective-permute-start.7
  28.6 0.8 %collective-permute-start.6 = (bf16[4,2,16,128]{3,2,1,0:T(8,128)(2,1)S(1)}, bf16[4,2,16,128]{3,2,1,0:T(8,128)(2,1)S(1)}, u32[]{:S(2)}, u32[]{:S(2)}) collective-permute-start(bf16[4,2,16,128]{3,2,1,0:T(8,128)(2,1)S(1)} %total.1.refs_0_), channel_id=1, source_target_pairs={{0,8},{8,0},{16,24},{24,16},{1,9},{9,1},{17,25},{25,17},{2,10},{10... | collective-permute-start | bytes 98312 | tf_op jit(solution)/shard_map/ppermute | solution.py:602
  29.4 1.4 %collective-permute-done.8.refs_3_ = bf16[4,2,16,128]{3,2,1,0:T(8,128)(2,1)S(1)} collective-permute-done((bf16[4,2,16,128]{3,2,1,0:T(8,128)(2,1)S(1)}, bf16[4,2,16,128]{3,2,1,0:T(8,128)(2,1)S(1)}, u32[]{:S(2)}, u32[]{:S(2)}) %collective-permute-start.8) | collective-permute-done | bytes 32800 | tf_op jit(solution)/shard_map/ppermute | solution.py:602
  30.8 2.6 %collective-permute-done.7.refs_2_ = bf16[4,2,16,128]{3,2,1,0:T(8,128)(2,1)S(1)} collective-permute-done((bf16[4,2,16,128]{3,2,1,0:T(8,128)(2,1)S(1)}, bf16[4,2,16,128]{3,2,1,0:T(8,128)(2,1)S(1)}, u32[]{:S(2)}, u32[]{:S(2)}) %collective-permute-start.7) | collective-permute-done | bytes 32800 | tf_op jit(solution)/shard_map/ppermute | solution.py:602
  33.4 0.0 collective-permute-done.6.refs_1_
  33.4 0.0 copy-done
  33.4 1.5 %dress.1 = bf16[4,18,2,16,128]{4,3,2,1,0:T(8,128)(2,1)} custom-call(s32[1,128]{1,0:T(1,128)S(1)} %get-tuple-element.24.table_any, bf16[8,2,128,128]{3,2,1,0:T(8,128)(2,1)S(1)} %bitcast.16, bf16[4,2,16,128]{3,2,1,0:T(8,128)(2,1)S(1)} %total.1.refs_0_, bf16[4,2,16,128]{3,2,1,0:T(8,128)(2,1)S(1)} %collective-permute-done.6.refs_1_, ...), custom_call_target="tpu_custom_call" | custom-call | flops 1000000000 | bytes 2000000 | tf_op jit(solution)/shard_map/dress/pallas_call | solution.py:537
  (5 shorter events, 0.1 us)
Async XLA Ops:
  1.8 13.4 %collective-permute-start = (bf16[2,6,96,128]{3,2,1,0:T(8,128)(2,1)S(1)}, bf16[2,6,96,128]{3,2,1,0:T(8,128)(2,1)S(1)}, u32[]{:S(2)}, u32[]{:S(2)}) collective-permute-start(bf16[2,6,96,128]{3,2,1,0:T(8,128)(2,1)S(1)} %get-tuple-element.25), channel_id=1, source_target_pairs={{0,1},{1,2},{2,3},{3,4},{4,5},{5,6},{6,7},{7,0},{8,9},{9,10},{10,1... | collective-permute-start | bytes 884744 | tf_op jit(solution)/shard_map/ppermute | solution.py:583
  2.4 5.0 %copy-start.1 = (s32[96,1]{0,1:T(1,128)S(1)}, s32[96,1]{0,1:T(1,128)}, u32[]{:S(2)}) copy-start(s32[96,1]{0,1:T(1,128)} %param.11) | copy-start | bytes 1156
  2.4 5.0 %copy-start.2 = (s32[96]{0:T(128)S(1)}, s32[96]{0:T(128)}, u32[]{:S(2)}) copy-start(s32[96]{0:T(128)} %param.12) | copy-start | bytes 1156
  2.4 5.0 %copy-start.3 = (s32[96]{0:T(128)S(1)}, s32[96]{0:T(128)}, u32[]{:S(2)}) copy-start(s32[96]{0:T(128)} %param.13) | copy-start | bytes 1156
  2.4 5.0 %copy-start.4 = (s32[96]{0:T(128)S(1)}, s32[96]{0:T(128)}, u32[]{:S(2)}) copy-start(s32[96]{0:T(128)} %param.14) | copy-start | bytes 1156
  2.4 5.0 %copy-start.5 = (f32[1,64]{1,0:T(1,128)S(1)}, f32[1,64]{1,0:T(1,128)}, u32[]{:S(2)}) copy-start(f32[1,64]{1,0:T(1,128)} %constant.2.clone.phase_ref) | copy-start | bytes 772
  4.7 10.5 %collective-permute-start.1 = (bf16[2,6,160,128]{3,2,1,0:T(8,128)(2,1)S(1)}, bf16[2,6,160,128]{3,2,1,0:T(8,128)(2,1)S(1)}, u32[]{:S(2)}, u32[]{:S(2)}) collective-permute-start(bf16[2,6,160,128]{3,2,1,0:T(8,128)(2,1)S(1)} %get-tuple-element.26), channel_id=1, source_target_pairs={{0,1},{1,2},{2,3},{3,4},{4,5},{5,6},{6,7},{7,0},{8,9},{9,10},{10,1... | collective-permute-start | bytes 1474568 | tf_op jit(solution)/shard_map/ppermute | solution.py:585
  15.2 18.2 %copy-start = (bf16[2,4,2,128,128]{4,3,2,1,0:T(8,128)(2,1)S(1)}, bf16[2,4,2,128,128]{4,3,2,1,0:T(8,128)(2,1)}, u32[]{:S(2)}) copy-start(bf16[2,4,2,128,128]{4,3,2,1,0:T(8,128)(2,1)} %param.10) | copy-start | bytes 1572868
  15.7 1.6 %collective-permute-start.2 = (f32[4,4,2,16,128]{4,3,2,1,0:T(8,128)S(1)}, f32[4,4,2,16,128]{4,3,2,1,0:T(8,128)S(1)}, u32[]{:S(2)}, u32[]{:S(2)}) collective-permute-start(f32[4,4,2,16,128]{4,3,2,1,0:T(8,128)S(1)} %get-tuple-element.30), channel_id=1, source_target_pairs={{0,1},{1,0},{2,3},{3,2},{4,5},{5,4},{6,7},{7,6},{8,9},{9,8},{10,11... | collective-permute-start | bytes 786440 | tf_op jit(solution)/shard_map/ppermute | solution.py:591
  17.4 4.1 %collective-permute-start.3 = (bf16[5,2,16,128]{3,2,1,0:T(8,128)(2,1)S(1)}, bf16[5,2,16,128]{3,2,1,0:T(8,128)(2,1)S(1)}, u32[]{:S(2)}, u32[]{:S(2)}) collective-permute-start(bf16[5,2,16,128]{3,2,1,0:T(8,128)(2,1)S(1)} %get-tuple-element.32), channel_id=1, source_target_pairs={{0,2},{1,3},{2,0},{3,1},{4,6},{5,7},{6,4},{7,5},{8,10},{9,11},{10,... | collective-permute-start | bytes 122888 | tf_op jit(solution)/shard_map/ppermute | solution.py:597
  18.9 4.0 %collective-permute-start.4 = (bf16[5,2,16,128]{3,2,1,0:T(8,128)(2,1)S(1)}, bf16[5,2,16,128]{3,2,1,0:T(8,128)(2,1)S(1)}, u32[]{:S(2)}, u32[]{:S(2)}) collective-permute-start(bf16[5,2,16,128]{3,2,1,0:T(8,128)(2,1)S(1)} %get-tuple-element.33), channel_id=1, source_target_pairs={{0,4},{1,5},{2,6},{3,7},{4,0},{5,1},{6,2},{7,3},{8,12},{9,13},{10,... | collective-permute-start | bytes 122888 | tf_op jit(solution)/shard_map/ppermute | solution.py:597
  20.0 4.9 %collective-permute-start.5 = (bf16[5,2,16,128]{3,2,1,0:T(8,128)(2,1)S(1)}, bf16[5,2,16,128]{3,2,1,0:T(8,128)(2,1)S(1)}, u32[]{:S(2)}, u32[]{:S(2)}) collective-permute-start(bf16[5,2,16,128]{3,2,1,0:T(8,128)(2,1)S(1)} %get-tuple-element.34), channel_id=1, source_target_pairs={{0,6},{1,7},{2,4},{3,5},{4,2},{5,3},{6,0},{7,1},{8,14},{9,15},{10,... | collective-permute-start | bytes 122888 | tf_op jit(solution)/shard_map/ppermute | solution.py:597
  24.9 5.9 %collective-permute-start.8 = (bf16[4,2,16,128]{3,2,1,0:T(8,128)(2,1)S(1)}, bf16[4,2,16,128]{3,2,1,0:T(8,128)(2,1)S(1)}, u32[]{:S(2)}, u32[]{:S(2)}) collective-permute-start(bf16[4,2,16,128]{3,2,1,0:T(8,128)(2,1)S(1)} %total.1.refs_0_), channel_id=1, source_target_pairs={{0,24},{8,16},{16,8},{24,0},{1,25},{9,17},{17,9},{25,1},{2,26},{10... | collective-permute-start | bytes 98312 | tf_op jit(solution)/shard_map/ppermute | solution.py:602
  28.6 4.8 %collective-permute-start.7 = (bf16[4,2,16,128]{3,2,1,0:T(8,128)(2,1)S(1)}, bf16[4,2,16,128]{3,2,1,0:T(8,128)(2,1)S(1)}, u32[]{:S(2)}, u32[]{:S(2)}) collective-permute-start(bf16[4,2,16,128]{3,2,1,0:T(8,128)(2,1)S(1)} %total.1.refs_0_), channel_id=1, source_target_pairs={{0,16},{8,24},{16,0},{24,8},{1,17},{9,25},{17,1},{25,9},{2,18},{10... | collective-permute-start | bytes 98312 | tf_op jit(solution)/shard_map/ppermute | solution.py:602
  28.6 4.8 %collective-permute-start.6 = (bf16[4,2,16,128]{3,2,1,0:T(8,128)(2,1)S(1)}, bf16[4,2,16,128]{3,2,1,0:T(8,128)(2,1)S(1)}, u32[]{:S(2)}, u32[]{:S(2)}) collective-permute-start(bf16[4,2,16,128]{3,2,1,0:T(8,128)(2,1)S(1)} %total.1.refs_0_), channel_id=1, source_target_pairs={{0,8},{8,0},{16,24},{24,16},{1,9},{9,1},{17,25},{25,17},{2,10},{10... | collective-permute-start | bytes 98312 | tf_op jit(solution)/shard_map/ppermute | solution.py:602
